TPU v7x, 32 devices: a whole 2x2x4 slice. The times are simulated.
32 devices in a mesh: gx: 8 (over z, x), gy: 4 (over y, core).
Axes of the slice: x: 2, y: 2, z: 4, core: 2. Of those that a mesh axis runs over, the one named last changes fastest.
Arguments:
- parcel_props: float32 [16, 131072], P(None, ('gx', 'gy')), may hold values from -6 to 6
- size_class: int32 [131072], P(('gx', 'gy')), may hold values from 0 to 7
- dest_owner: int32 [131072, 1], P(('gx', 'gy')), may hold values from 0 to 31; in each aligned block of 4096 rows (0 to 4095, 4096 to 8191, ...) at most 512 rows name the same one
- dest_local: int32 [131072], P(('gx', 'gy')), may hold values from 0 to 4095
- class_table: float32 [8, 16], replicated, may hold values from 0.5 to 2
- gas_density: float32 [256, 512], P('gx', 'gy'), may hold values from 0.5 to 2
- gas_rest: float32 [4, 256, 512], P(None, 'gx', 'gy'), may hold values from -6 to 6
Outputs:
- new_density: float32 [256, 512], P('gx', 'gy')
- new_rest: float32 [4, 256, 512], P(None, 'gx', 'gy')
Inputs may be any that keep to these rules, and one draw needn't show every extreme that they name: `dest_owner`: among the parcels of one device, no owner device is named by more than 512 of them, a bound that some block reaches.
All inputs are finite; a program needn't handle non-finite values.
Results may differ from a plain program's by a relative error of at most 0.00015.
Values sent between devices are 32-bit elements; how exact they have to be, the bound alone decides.
A program may use at most 64 MiB of HBM per device.

v0:
```python
import functools

import jax
import jax.numpy as jnp
from jax import lax
from jax.experimental import pallas as pl
from jax.experimental.pallas import tpu as pltpu
from jax.sharding import PartitionSpec as P

F32 = jnp.float32
BF16 = jnp.bfloat16
LANES = 128
ROWS = 8
BATCH = 16
NT = (((1,), (1,)), ((), ()))


def split(x):
    high = x.astype(BF16).astype(F32)
    return high, x - high


def iota(shape, dim):
    return lax.broadcasted_iota(jnp.int32, shape, dim)


def fused_kernel(
    width_x,
    width_y,
    capacity,
    props_ref,
    class_ref,
    owner_ref,
    cell_ref,
    table_ref,
    scalars_ref,
    dens_ref,
    rest_ref,
    smooth_ref,
    hot,
    vals,
    owners,
    packed,
    got,
    spot,
    gas,
    src,
    total,
    row_out,
    row_in,
    col_out,
    col_in,
    send_sem,
    recv_sem,
    halo_send,
    halo_recv,
):
    devices = width_x * width_y
    groups = devices // ROWS
    batch = BATCH
    my_x, my_y = lax.axis_index("gx"), lax.axis_index("gy")
    me = my_x * width_y + my_y
    props_count, parcels = props_ref.shape
    classes = table_ref.shape[0]
    slab_x, slab_y = dens_ref.shape

    def place(device):
        return (device // width_y, device % width_y)

    barrier = pltpu.get_barrier_semaphore()

    def greet(k, unused):
        pl.semaphore_signal(
            barrier,
            inc=1,
            device_id=place((me + k) % devices),
            device_id_type=pl.DeviceIdType.MESH,
        )
        return unused

    lax.fori_loop(1, devices, greet, 0)

    def group_at(step):
        turn = (1 - 2 * (step % 2)) * ((step + 1) // 2)
        return (me // ROWS + groups // 2 + turn + groups) % groups

    def copy_to(device):
        return pltpu.make_async_remote_copy(
            src_ref=packed.at[device],
            dst_ref=got.at[me],
            send_sem=send_sem.at[device],
            recv_sem=recv_sem.at[me],
            device_id=place(device),
            device_id_type=pl.DeviceIdType.MESH,
        )

    def copy_from(device):
        return pltpu.make_async_remote_copy(
            src_ref=packed.at[device],
            dst_ref=got.at[device],
            send_sem=send_sem.at[device],
            recv_sem=recv_sem.at[device],
            device_id=place(device),
            device_id_type=pl.DeviceIdType.MESH,
        )

    row, col = (iota((LANES, 2 * LANES), 0), iota((LANES, 2 * LANES), 1))
    upper = jnp.where((col >= LANES) | (row < col), 1.0, 0.0).astype(BF16)
    ids = iota((devices, LANES), 0)
    wide = min(capacity, 256)
    ranks = iota((wide, LANES), 0).astype(F32).astype(BF16)
    one, zero = jnp.ones((), BF16), jnp.zeros((), BF16)
    carry = jnp.zeros((devices, LANES), F32)
    for c in range(parcels // LANES):
        mine = owner_ref[:, c * LANES : (c + 1) * LANES] == ids
        counted = jnp.dot(
            jnp.where(mine, 1.0, 0.0).astype(BF16), upper, preferred_element_type=F32
        )
        rank = jnp.sum(
            jnp.where(mine, counted[:, :LANES] + carry, 0.0), axis=0, keepdims=True
        )
        carry = carry + counted[:, LANES:]
        for start in range(0, capacity, wide):
            local = jnp.clip(rank - start, -1.0, 256.0).astype(BF16)
            hot[start : start + wide, c * LANES : (c + 1) * LANES] = jnp.where(
                ranks == local, one, zero
            )

    eye = jnp.where(
        iota((props_count, props_count), 0) == iota((props_count, props_count), 1), 1.0, 0.0
    ).astype(BF16)
    table = jnp.concatenate(split(table_ref[...]), axis=0).astype(BF16)
    turned = lax.dot_general(eye, table, NT, preferred_element_type=F32).astype(BF16)
    picks = jnp.where(class_ref[...] == iota((classes, parcels), 0), 1.0, 0.0)
    picks = jnp.concatenate([picks, picks], axis=0).astype(BF16)
    coef = jnp.dot(turned, picks, preferred_element_type=F32)
    props = props_ref[...]
    which = iota((props_count, parcels), 0)
    weights = jnp.where(which >= 5, coef, jnp.where(which == 4, 1.0, 0.0))
    heat_sum = jnp.sum(weights * props, axis=0, keepdims=True)
    which = iota((ROWS, parcels), 0)
    mixed = jnp.where(which == 0, jnp.exp(0.5 * props[0:1]), props[0:ROWS])
    mixed = jnp.where(which == 5, heat_sum, mixed)
    mixed = jnp.where(which == 6, class_ref[...].astype(F32), mixed)
    mixed = jnp.where(which == 7, cell_ref[...].astype(F32), mixed)
    vals[...] = jnp.concatenate(split(mixed), axis=0).astype(BF16)
    owners[...] = jnp.broadcast_to(
        owner_ref[...].astype(F32), (2 * ROWS, parcels)
    ).astype(BF16)

    pl.semaphore_wait(barrier, devices - 1)

    def send_group(step, unused):
        first = (me // batch + devices // batch // 2 + step) % (devices // batch) * batch
        sends = [
            jnp.where(
                owners[...] == (first + i).astype(F32).astype(BF16), vals[...], zero
            )
            for i in range(batch)
        ]
        both = lax.dot_general(
            jnp.concatenate(sends, axis=0), hot[...], NT, preferred_element_type=F32
        )
        for i in range(batch):
            at = 2 * ROWS * i
            packed[first + i] = both[at : at + ROWS] + both[at + ROWS : at + 2 * ROWS]

        def launch(i, carried):
            device = first + i

            @pl.when(device != me)
            def _():
                copy_to(device).start()

            return carried

        return lax.fori_loop(0, batch, launch, unused)

    lax.fori_loop(0, devices // batch, send_group, 0)
    got[me] = packed[me]

    fields = jnp.concatenate([dens_ref[...], rest_ref[...].reshape(4 * slab_x, slab_y)], axis=0)
    tab = jnp.concatenate(split(fields), axis=1).astype(BF16)
    total[...] = jnp.zeros_like(total)
    ys = iota((slab_y, capacity), 0).astype(F32).astype(BF16)
    xs = iota((slab_x, capacity), 0)

    def take_group(step, unused):
        first = group_at(step) * ROWS

        def arrive(i, carried):
            @pl.when(first + i != me)
            def _():
                copy_from(first + i).wait_recv()

            return carried

        lax.fori_loop(0, ROWS, arrive, 0)

        def cell_of(i):
            return got[first + i][7:8].astype(jnp.int32)

        def part(c):
            return jnp.concatenate([got[first + i][c : c + 1] for i in range(ROWS)], axis=0)

        for i in range(ROWS):
            cell = cell_of(i)
            lane_hot = jnp.where(
                ys == (cell % slab_y).astype(F32).astype(BF16), one, zero
            )
            spot[:, i * capacity : (i + 1) * capacity] = lane_hot
            found = jnp.dot(
                tab, jnp.concatenate([lane_hot, lane_hot], axis=0), preferred_element_type=F32
            )
            in_row = xs == cell // slab_y
            for c in range(5):
                gas[c, i : i + 1] = jnp.sum(
                    jnp.where(in_row, found[c * slab_x : (c + 1) * slab_x], 0.0),
                    axis=0,
                    keepdims=True,
                )

        kind = part(6).astype(jnp.int32)
        coefs = [jnp.full(kind.shape, scalars_ref[0, j], F32) for j in range(5)]
        for k in range(1, classes):
            same = kind == k
            coefs = [jnp.where(same, scalars_ref[k, j], coefs[j]) for j in range(5)]
        mass = part(0)
        speed = [part(j) for j in (1, 2, 3)]
        heat, energy = part(4), part(5)
        inverse = 1.0 / gas[0]
        slip = [speed[j] - gas[j + 1] * inverse for j in range(3)]
        excess = heat - gas[4] * inverse
        soft = jnp.maximum(excess, 0.0) + jnp.log1p(jnp.exp(-jnp.abs(excess)))
        evapor = mass * (1.0 - jnp.exp(-(coefs[0] * soft)))
        square = slip[0] * slip[0] + slip[1] * slip[1] + slip[2] * slip[2]
        drag = mass * (1.0 - jnp.exp(-coefs[1] * jnp.sqrt(1.0 + square)))
        out = [evapor]
        out += [evapor * coefs[2 + j] * speed[j] + drag * slip[j] for j in range(3)]
        out += [evapor * energy]
        for c in range(5):
            high, low = split(out[c])
            src[c] = high
            src[5 + c] = low

        for i in range(ROWS):
            in_row = xs == cell_of(i) // slab_y
            spread = [jnp.where(in_row, src[c, i : i + 1], 0.0).astype(BF16) for c in range(10)]
            total[...] += lax.dot_general(
                jnp.concatenate(spread, axis=0),
                spot[:, i * capacity : (i + 1) * capacity],
                NT,
                preferred_element_type=F32,
            )
        return unused

    lax.fori_loop(0, groups, take_group, 0)

    half = 5 * slab_x
    deposit = [
        total[c * slab_x : (c + 1) * slab_x]
        + total[half + c * slab_x : half + (c + 1) * slab_x]
        for c in range(5)
    ]
    lane = iota((slab_x, slab_y), 1)
    low_edge = jnp.zeros((slab_x, slab_y), F32)
    high_edge = jnp.zeros((slab_x, slab_y), F32)
    row_out[...] = jnp.zeros_like(row_out)
    for c in range(5):
        row_out[0, c : c + 1] = deposit[c][0:1]
        row_out[1, c : c + 1] = deposit[c][slab_x - 1 : slab_x]
        low_edge = jnp.where(
            lane == c, pltpu.roll(deposit[c], c, 1) if c else deposit[c], low_edge
        )
        high_edge = jnp.where(lane == c, pltpu.roll(deposit[c], c + 1, 1), high_edge)
    col_out[0] = low_edge
    col_out[1] = high_edge

    def edge(out_ref, in_ref, side, base, target):
        return pltpu.make_async_remote_copy(
            src_ref=out_ref.at[side],
            dst_ref=in_ref.at[side],
            send_sem=halo_send.at[base + side],
            recv_sem=halo_recv.at[base + side],
            device_id=target,
            device_id_type=pl.DeviceIdType.MESH,
        )

    edges = [
        (row_out, row_in, 0, 0, (my_x - 1, my_y), my_x > 0, my_x < width_x - 1),
        (row_out, row_in, 1, 0, (my_x + 1, my_y), my_x < width_x - 1, my_x > 0),
        (col_out, col_in, 0, 2, (my_x, my_y - 1), my_y > 0, my_y < width_y - 1),
        (col_out, col_in, 1, 2, (my_x, my_y + 1), my_y < width_y - 1, my_y > 0),
    ]
    for out_ref, in_ref, side, base, target, sends, takes in edges:

        @pl.when(sends)
        def _(out_ref=out_ref, in_ref=in_ref, side=side, base=base, target=target):
            edge(out_ref, in_ref, side, base, target).start()

        @pl.when(jnp.logical_not(takes))
        def _(in_ref=in_ref, side=side):
            in_ref[side] = jnp.zeros(in_ref.shape[1:], F32)

    def wait_sent(k, unused):
        copy_to((me + k) % devices).wait_send()
        return unused

    lax.fori_loop(1, devices, wait_sent, 0)
    for out_ref, in_ref, side, base, target, sends, takes in edges:

        @pl.when(takes)
        def _(out_ref=out_ref, in_ref=in_ref, side=side, base=base, target=target):
            edge(out_ref, in_ref, side, base, target).wait_recv()

    for c in range(5):
        here = deposit[c]
        above = jnp.concatenate([row_in[1, c : c + 1], here[: slab_x - 1]], axis=0)
        below = jnp.concatenate([here[1:], row_in[0, c : c + 1]], axis=0)
        left_in = pltpu.roll(col_in[1], slab_y - c, 1) if c else col_in[1]
        left = jnp.where(lane == 0, left_in, pltpu.roll(here, 1, 1))
        right = jnp.where(
            lane == slab_y - 1,
            pltpu.roll(col_in[0], slab_y - 1 - c, 1),
            pltpu.roll(here, slab_y - 1, 1),
        )
        smooth = 0.4 * here + 0.15 * (below + above + right + left)
        smooth_ref[c] = smooth

    for out_ref, in_ref, side, base, target, sends, takes in edges:

        @pl.when(sends)
        def _(out_ref=out_ref, in_ref=in_ref, side=side, base=base, target=target):
            edge(out_ref, in_ref, side, base, target).wait_send()


def per_device(
    parcel_props, size_class, dest_owner, dest_local, class_table, gas_density, gas_rest
):
    width_x, width_y = lax.axis_size("gx"), lax.axis_size("gy")
    devices = width_x * width_y
    props_count, parcels = parcel_props.shape
    slab_x, slab_y = gas_density.shape
    capacity = -(-max(2, 4 * parcels // devices) // LANES) * LANES
    vmem = pl.BlockSpec(memory_space=pltpu.VMEM)
    smem = pl.BlockSpec(memory_space=pltpu.SMEM)
    smooth = pl.pallas_call(
        functools.partial(fused_kernel, width_x, width_y, capacity),
        out_shape=jax.ShapeDtypeStruct((5, slab_x, slab_y), F32),
        in_specs=[vmem] * 5 + [smem] + [vmem] * 2,
        out_specs=vmem,
        scratch_shapes=[
            pltpu.VMEM((capacity, parcels), BF16),
            pltpu.VMEM((2 * ROWS, parcels), BF16),
            pltpu.VMEM((2 * ROWS, parcels), BF16),
            pltpu.VMEM((devices, ROWS, capacity), F32),
            pltpu.VMEM((devices, ROWS, capacity), F32),
            pltpu.VMEM((slab_y, ROWS * capacity), BF16),
            pltpu.VMEM((5, ROWS, capacity), F32),
            pltpu.VMEM((10, ROWS, capacity), F32),
            pltpu.VMEM((10 * slab_x, slab_y), F32),
            pltpu.VMEM((2, ROWS, slab_y), F32),
            pltpu.VMEM((2, ROWS, slab_y), F32),
            pltpu.VMEM((2, slab_x, slab_y), F32),
            pltpu.VMEM((2, slab_x, slab_y), F32),
            pltpu.SemaphoreType.DMA((devices,)),
            pltpu.SemaphoreType.DMA((devices,)),
            pltpu.SemaphoreType.DMA((4,)),
            pltpu.SemaphoreType.DMA((4,)),
        ],
        compiler_params=pltpu.CompilerParams(collective_id=0, has_side_effects=True),
    )(
        parcel_props,
        size_class.reshape(1, parcels),
        dest_owner.reshape(1, parcels),
        dest_local.reshape(1, parcels),
        class_table,
        class_table,
        gas_density,
        gas_rest,
    )
    return (gas_density + smooth[0], gas_rest + smooth[1:])


def solution(mesh):
    return jax.shard_map(
        per_device,
        mesh=mesh,
        in_specs=(
            P(None, ("gx", "gy")),
            P(("gx", "gy")),
            P(("gx", "gy"), None),
            P(("gx", "gy")),
            P(),
            P("gx", "gy"),
            P(None, "gx", "gy"),
        ),
        out_specs=(P("gx", "gy"), P(None, "gx", "gy")),
        check_vma=False,
    )
```

profile of v0, /device:TPU:27, one launch (start us, length us, event | category | flops | bytes accessed | tf_op | source)
XLA Modules:
  0.0 34.4 jit_solution(6313935690390311471)
XLA Ops:
  0.6 0.0 copy-start.1
  0.6 0.0 copy-start
  0.7 31.0 %shard_map.86 = f32[5,32,128]{2,1,0:T(8,128)} custom-call(f32[16,4096]{1,0:T(8,128)} %props_ref.1, s32[1,4096]{1,0:T(1,128)} %bitcast.5, s32[1,4096]{1,0:T(1,128)} %bitcast.6, s32[1,4096]{1,0:T(1,128)} %bitcast.7, f32[8,16]{1,0:T(8,128)} %scalars_ref.1, f32[8,16]{1,0:T(8,128)} %scalars_ref.1, f32[32,128]{1,0:T(8,128)} %dens_ref.1, f32[4,32,128]{2,1,0:T(8,128)} %rest_ref.1), custom_call_target="tpu_custom_call" | custom-call | tf_op jit(solution)/shard_map/pallas_call | solution.py:347
  31.6 0.0 copy-done.1
  31.6 1.3 %bitcast_add_fusion = f32[32,128]{1,0:T(8,128)} fusion(f32[32,128]{1,0:T(8,128)S(1)} %copy-done.1, f32[5,32,128]{2,1,0:T(8,128)} %shard_map.86), kind=kLoop, calls=%fused_computation.1 | loop fusion | flops 4096 | bytes 49152 | tf_op jit(solution)/shard_map/add | solution.py:382
  32.9 0.0 copy-done
  33.0 1.5 %slice_add_fusion = f32[4,32,128]{2,1,0:T(8,128)} fusion(f32[4,32,128]{2,1,0:T(8,128)S(1)} %copy-done, f32[5,32,128]{2,1,0:T(8,128)} %shard_map.86), kind=kLoop, calls=%fused_computation | loop fusion | flops 16384 | bytes 196608 | tf_op jit(solution)/shard_map/add | solution.py:382
Async XLA Ops:
  0.6 31.0 %copy-start.1 = (f32[32,128]{1,0:T(8,128)S(1)}, f32[32,128]{1,0:T(8,128)}, u32[]{:S(2)}) copy-start(f32[32,128]{1,0:T(8,128)} %dens_ref.1) | copy-start | bytes 49156
  0.6 32.3 %copy-start = (f32[4,32,128]{2,1,0:T(8,128)S(1)}, f32[4,32,128]{2,1,0:T(8,128)}, u32[]{:S(2)}) copy-start(f32[4,32,128]{2,1,0:T(8,128)} %rest_ref.1) | copy-start | bytes 196612
where the time goes:
time: 34.7 us; the launch traced here: 34.4 us
  Pallas kernels  31 us (89%)
  other arithmetic  2.8 us (8%)
  between operations  0.66 us (2%)
    pallas_call x1, Pallas kernels, per_device(): pl.pallas_call(functools.partial(fused_kernel, width_x, width_y, capacity...  31 us
    add x2, other arithmetic, per_device(): return (gas_density + smooth[0], gas_rest + smooth[1:])  2.8 us

commit v1 on v0

v1 whole, which is shorter than its diff:
```python
import functools

import jax
import jax.numpy as jnp
from jax import lax
from jax.experimental import pallas as pl
from jax.experimental.pallas import tpu as pltpu
from jax.sharding import PartitionSpec as P

F32 = jnp.float32
BF16 = jnp.bfloat16
LANES = 128
ROWS = 8
BATCH = 16
NT = (((1,), (1,)), ((), ()))
MESH = pl.DeviceIdType.MESH


def split(x):
    high = x.astype(BF16).astype(F32)
    return high, x - high


def iota(shape, dim):
    return lax.broadcasted_iota(jnp.int32, shape, dim)


def loop(count, body):
    if count <= 2:
        for step in range(count):
            body(step)
    else:
        lax.fori_loop(0, count, lambda step, unused: (body(step), unused)[1], 0)


def fused_kernel(
    width_x,
    width_y,
    capacity,
    props_hbm,
    class_hbm,
    owner_hbm,
    cell_hbm,
    table_hbm,
    dens_hbm,
    rest_hbm,
    dens_out,
    rest_out,
    props_ref,
    class_ref,
    owner_ref,
    cell_ref,
    table_ref,
    scalars_ref,
    field,
    far_field,
    hot,
    vals,
    keys,
    packed,
    got,
    spot,
    gas,
    tab,
    total,
    far_out,
    far_in,
    row_out,
    row_in,
    col_out,
    col_in,
    load_sem,
    send_sem,
    recv_sem,
    far_send,
    far_recv,
    halo_send,
    halo_recv,
):
    devices = width_x * width_y
    deep = width_x // 2
    team = deep * width_y
    groups = team // ROWS
    my_x, my_y = lax.axis_index("gx"), lax.axis_index("gy")
    half = lax.div(my_x, deep)
    row_of = my_x - half * deep
    me = row_of * width_y + my_y
    base_x = half * deep
    mirror = (row_of + (1 - half) * deep, my_y)
    props_count, parcels = props_ref.shape
    classes = table_ref.shape[0]
    slab_x, slab_y = dens_hbm.shape

    def mate(local):
        return (base_x + lax.div(local, width_y), lax.rem(local, width_y))

    loads = [
        pltpu.make_async_copy(a, b, load_sem.at[i])
        for i, (a, b) in enumerate(
            [
                (owner_hbm, owner_ref),
                (dens_hbm, field.at[0]),
                (rest_hbm, field.at[1:5]),
                (table_hbm, table_ref),
                (class_hbm, class_ref),
                (cell_hbm, cell_ref),
                (props_hbm, props_ref),
                (table_hbm, scalars_ref),
            ]
        )
    ]
    for load in loads:
        load.start()

    barrier = pltpu.get_barrier_semaphore()

    def greet(target):
        pl.semaphore_signal(barrier, inc=1, device_id=target, device_id_type=MESH)

    greet(mirror)
    last_low = (half == 0) & (row_of == deep - 1)
    first_high = (half == 1) & (row_of == 0)

    @pl.when(last_low)
    def _():
        greet((my_x + 1, my_y))

    @pl.when(first_high)
    def _():
        greet((my_x - 1, my_y))

    def greet_mate(k, unused):
        greet(mate(lax.rem(me + k, team)))
        return unused

    lax.fori_loop(1, team, greet_mate, 0, unroll=5 if team == 16 else 1)
    border = jnp.where(last_low | first_high, 1, 0)

    def copy_to(phase, local):
        return pltpu.make_async_remote_copy(
            src_ref=packed.at[phase, local],
            dst_ref=got.at[phase, me],
            send_sem=send_sem.at[phase, local],
            recv_sem=recv_sem.at[phase, me],
            device_id=mate(local),
            device_id_type=MESH,
        )

    def copy_from(phase, local):
        return pltpu.make_async_remote_copy(
            src_ref=packed.at[phase, local],
            dst_ref=got.at[phase, local],
            send_sem=send_sem.at[phase, local],
            recv_sem=recv_sem.at[phase, local],
            device_id=mate(local),
            device_id_type=MESH,
        )

    def far_copy(out_ref, in_ref, i):
        return pltpu.make_async_remote_copy(
            src_ref=out_ref,
            dst_ref=in_ref,
            send_sem=far_send.at[i],
            recv_sem=far_recv.at[i],
            device_id=mirror,
            device_id_type=MESH,
        )

    loads[0].wait()
    row, col = (iota((LANES, 2 * LANES), 0), iota((LANES, 2 * LANES), 1))
    upper = jnp.where((col >= LANES) | (row < col), 1.0, 0.0).astype(BF16)
    ids = iota((devices, LANES), 0)
    wide = hot.shape[0]
    spans = capacity // wide
    ranks = iota((wide, LANES), 0).astype(F32).astype(BF16)
    one, zero = jnp.ones((), BF16), jnp.zeros((), BF16)
    carry = jnp.zeros((devices, LANES), F32)
    chunks = parcels // LANES
    for start in range(0, chunks, ROWS):
        span = range(start, min(start + ROWS, chunks))
        named = [owner_ref[:, c * LANES : (c + 1) * LANES] for c in span]
        mine = [jnp.where(owner == ids, 1.0, 0.0) for owner in named]
        counted = jnp.dot(
            jnp.concatenate(mine, axis=0).astype(BF16), upper, preferred_element_type=F32
        )
        for i, c in enumerate(span):
            part_of = counted[i * devices : (i + 1) * devices]
            rank = jnp.sum(mine[i] * (part_of[:, :LANES] + carry), axis=0, keepdims=True)
            carry = carry + part_of[:, LANES:]
            key = named[i].astype(F32)
            if spans > 1:
                level = sum(jnp.where(rank >= wide * k, 1.0, 0.0) for k in range(1, spans))
                rank = rank - level * wide
                key = key * spans + level
            at = slice(c * LANES, (c + 1) * LANES)
            keys[:, at] = jnp.broadcast_to(key, (2 * ROWS, LANES)).astype(BF16)
            hot[:, at] = jnp.where(ranks == rank.astype(BF16), one, zero)

    for load in loads[1:]:
        load.wait()
    eye = jnp.where(
        iota((props_count, props_count), 0) == iota((props_count, props_count), 1), 1.0, 0.0
    ).astype(BF16)
    table = jnp.concatenate(split(table_ref[...]), axis=0).astype(BF16)
    turned = lax.dot_general(eye, table, NT, preferred_element_type=F32).astype(BF16)
    picks = jnp.where(class_ref[...] == iota((classes, parcels), 0), 1.0, 0.0)
    picks = jnp.concatenate([picks, picks], axis=0).astype(BF16)
    coef = jnp.dot(turned, picks, preferred_element_type=F32)
    props = props_ref[...]
    which = iota((props_count, parcels), 0)
    weights = jnp.where(which >= 5, coef, jnp.where(which == 4, 1.0, 0.0))
    heat_sum = jnp.sum(weights * props, axis=0, keepdims=True)
    which = iota((ROWS, parcels), 0)
    mixed = jnp.where(which == 0, jnp.exp(0.5 * props[0:1]), props[0:ROWS])
    mixed = jnp.where(which == 5, heat_sum, mixed)
    mixed = jnp.where(which == 6, class_ref[...].astype(F32), mixed)
    mixed = jnp.where(which == 7, cell_ref[...].astype(F32), mixed)
    vals[...] = jnp.concatenate(split(mixed), axis=0).astype(BF16)

    pl.semaphore_wait(barrier, team + border)
    far_copy(field, far_field, 0).start()
    batches = team // BATCH

    def send_group(step):
        phase = step // batches
        first = (step % batches) * BATCH
        first_id = jnp.where(phase == half, team, 0) + first
        count = BATCH * spans // 2
        both = [0.0, 0.0]
        for start in range(0, parcels, 256):
            at = slice(start, start + 256)
            for side in range(2):
                sends = [
                    jnp.where(
                        keys[:, at]
                        == (first_id * spans + side * count + i).astype(F32).astype(BF16),
                        vals[:, at],
                        zero,
                    )
                    for i in range(count)
                ]
                both[side] += lax.dot_general(
                    jnp.concatenate(sends, axis=0),
                    hot[:, at],
                    NT,
                    preferred_element_type=F32,
                )
        both = jnp.concatenate(both, axis=0)
        for i in range(BATCH):
            for k in range(spans):
                at = 2 * ROWS * (i * spans + k)
                packed[phase, first + i, :, k * wide : (k + 1) * wide] = (
                    both[at : at + ROWS] + both[at + ROWS : at + 2 * ROWS]
                )

        def launch(i, carried):
            local = first + lax.rem(me + i, BATCH)

            @pl.when(local != me)
            def _():
                copy_to(phase, local).start()

            return carried

        lax.fori_loop(1, BATCH + 1, launch, 0, unroll=True)

    loop(2 * batches, send_group)
    for phase in range(2):
        got[phase, me] = packed[phase, me]

    half_x = slab_x // 2
    ys = iota((2 * slab_y, capacity), 0).astype(F32).astype(BF16)
    xs = iota((half_x, capacity), 0)
    xs_short = xs.astype(F32).astype(BF16)

    def run_phase(phase, fields):
        parts = []
        for c in range(5):
            for piece in split(fields[c]):
                parts.append(jnp.concatenate([piece[:half_x], piece[half_x:]], axis=1))
        tab[...] = jnp.concatenate(parts, axis=0).astype(BF16)
        total[...] = jnp.zeros_like(total)

        def take_group(step, unused):
            turn = lax.div(me, ROWS) + step
            first = lax.rem(turn, groups) * ROWS

            def arrive(i, carried):
                @pl.when(first + i != me)
                def _():
                    copy_from(phase, first + i).wait_recv()

                return carried

            lax.fori_loop(0, ROWS, arrive, 0, unroll=True)

            def part(c):
                return jnp.concatenate(
                    [got[phase, first + i][c : c + 1] for i in range(ROWS)], axis=0
                )

            cell = part(7).astype(jnp.int32)
            line = lax.div(cell, slab_y)
            upper_half = jnp.where(line >= half_x, 1, 0)
            lanes_at = (cell - line * slab_y + upper_half * slab_y).astype(F32)
            lines_at = line - upper_half * half_x
            lines_short = lines_at.astype(F32)
            for i in range(ROWS):
                spot_at = slice(i * capacity, (i + 1) * capacity)
                spot[:, spot_at] = jnp.where(
                    ys == lanes_at[i : i + 1].astype(BF16), one, zero
                )
                found = jnp.dot(tab[...], spot[:, spot_at], preferred_element_type=F32)
                in_row = xs == lines_at[i : i + 1]
                for c in range(5):
                    at = 2 * c * half_x
                    both = found[at : at + half_x] + found[at + half_x : at + 2 * half_x]
                    gas[c, i : i + 1] = jnp.sum(
                        jnp.where(in_row, both, 0.0), axis=0, keepdims=True
                    )

            kind = part(6).astype(jnp.int32)
            coefs = [jnp.full(kind.shape, scalars_ref[0, j], F32) for j in range(5)]
            for k in range(1, classes):
                same = kind == k
                coefs = [jnp.where(same, scalars_ref[k, j], coefs[j]) for j in range(5)]
            mass = part(0)
            speed = [part(j) for j in (1, 2, 3)]
            heat, energy = part(4), part(5)
            inverse = 1.0 / gas[0]
            slip = [speed[j] - gas[j + 1] * inverse for j in range(3)]
            excess = heat - gas[4] * inverse
            soft = jnp.maximum(excess, 0.0) + jnp.log1p(jnp.exp(-jnp.abs(excess)))
            evapor = mass * (1.0 - jnp.exp(-(coefs[0] * soft)))
            square = slip[0] * slip[0] + slip[1] * slip[1] + slip[2] * slip[2]
            drag = mass * (1.0 - jnp.exp(-coefs[1] * jnp.sqrt(1.0 + square)))
            out = [evapor]
            out += [evapor * coefs[2 + j] * speed[j] + drag * slip[j] for j in range(3)]
            out += [evapor * energy]

            pieces = [piece for c in range(5) for piece in split(out[c])]
            spread = []
            for i in range(ROWS):
                in_row = xs_short == lines_short[i : i + 1].astype(BF16)
                spread.append(
                    jnp.concatenate(
                        [
                            jnp.where(in_row, piece[i : i + 1].astype(BF16), zero)
                            for piece in pieces
                        ],
                        axis=0,
                    )
                )
            part_total = 0.0
            for at in (0, ROWS // 2):
                part_total += lax.dot_general(
                    jnp.concatenate(spread[at : at + ROWS // 2], axis=1),
                    spot[:, at * capacity : (at + ROWS // 2) * capacity],
                    NT,
                    preferred_element_type=F32,
                )
            total[...] += part_total
            return unused

        lax.fori_loop(0, groups, take_group, 0)
        summed = []
        for c in range(5):
            at = 2 * c * half_x
            both = total[at : at + half_x] + total[at + half_x : at + 2 * half_x]
            summed.append(jnp.concatenate([both[:, :slab_y], both[:, slab_y:]], axis=0))
        return summed

    far_copy(field, far_field, 0).wait_recv()
    for c, piece in enumerate(run_phase(0, far_field)):
        far_out[c] = piece
    far_copy(far_out, far_in, 1).start()
    mine = run_phase(1, field)
    far_copy(far_out, far_in, 1).wait_recv()
    deposit = [mine[c] + far_in[c] for c in range(5)]
    lane = iota((slab_x, slab_y), 1)
    low_edge = jnp.zeros((slab_x, slab_y), F32)
    high_edge = jnp.zeros((slab_x, slab_y), F32)
    row_out[...] = jnp.zeros_like(row_out)
    for c in range(5):
        row_out[0, c : c + 1] = deposit[c][0:1]
        row_out[1, c : c + 1] = deposit[c][slab_x - 1 : slab_x]
        low_edge = jnp.where(
            lane == c, pltpu.roll(deposit[c], c, 1) if c else deposit[c], low_edge
        )
        high_edge = jnp.where(lane == c, pltpu.roll(deposit[c], c + 1, 1), high_edge)
    col_out[0] = low_edge
    col_out[1] = high_edge

    def edge(out_ref, in_ref, side, base, target):
        return pltpu.make_async_remote_copy(
            src_ref=out_ref.at[side],
            dst_ref=in_ref.at[side],
            send_sem=halo_send.at[base + side],
            recv_sem=halo_recv.at[base + side],
            device_id=target,
            device_id_type=MESH,
        )

    edges = [
        (row_out, row_in, 0, 0, (my_x - 1, my_y), my_x > 0, my_x < width_x - 1),
        (row_out, row_in, 1, 0, (my_x + 1, my_y), my_x < width_x - 1, my_x > 0),
        (col_out, col_in, 0, 2, (my_x, my_y - 1), my_y > 0, my_y < width_y - 1),
        (col_out, col_in, 1, 2, (my_x, my_y + 1), my_y < width_y - 1, my_y > 0),
    ]
    for out_ref, in_ref, side, base, target, sends, takes in edges:

        @pl.when(sends)
        def _(out_ref=out_ref, in_ref=in_ref, side=side, base=base, target=target):
            edge(out_ref, in_ref, side, base, target).start()

        @pl.when(jnp.logical_not(takes))
        def _(in_ref=in_ref, side=side):
            in_ref[side] = jnp.zeros(in_ref.shape[1:], F32)

    def wait_sent(k, unused):
        local = lax.rem(me + k, team)
        for phase in range(2):
            copy_to(phase, local).wait_send()
        return unused

    lax.fori_loop(1, team, wait_sent, 0)
    far_copy(field, far_field, 0).wait_send()
    far_copy(far_out, far_in, 1).wait_send()
    for out_ref, in_ref, side, base, target, sends, takes in edges:

        @pl.when(takes)
        def _(out_ref=out_ref, in_ref=in_ref, side=side, base=base, target=target):
            edge(out_ref, in_ref, side, base, target).wait_recv()

    for c in range(5):
        here = deposit[c]
        above = jnp.concatenate([row_in[1, c : c + 1], here[: slab_x - 1]], axis=0)
        below = jnp.concatenate([here[1:], row_in[0, c : c + 1]], axis=0)
        left_in = pltpu.roll(col_in[1], slab_y - c, 1) if c else col_in[1]
        left = jnp.where(lane == 0, left_in, pltpu.roll(here, 1, 1))
        right = jnp.where(
            lane == slab_y - 1,
            pltpu.roll(col_in[0], slab_y - 1 - c, 1),
            pltpu.roll(here, slab_y - 1, 1),
        )
        smooth = 0.4 * here + 0.15 * (below + above + right + left)
        if c:
            rest_out[c - 1] = field[c] + smooth
        else:
            dens_out[...] = field[0] + smooth

    for out_ref, in_ref, side, base, target, sends, takes in edges:

        @pl.when(sends)
        def _(out_ref=out_ref, in_ref=in_ref, side=side, base=base, target=target):
            edge(out_ref, in_ref, side, base, target).wait_send()


def per_device(
    parcel_props, size_class, dest_owner, dest_local, class_table, gas_density, gas_rest
):
    width_x, width_y = lax.axis_size("gx"), lax.axis_size("gy")
    devices = width_x * width_y
    team = devices // 2
    props_count, parcels = parcel_props.shape
    slab_x, slab_y = gas_density.shape
    capacity = -(-max(2, 4 * parcels // devices) // LANES) * LANES
    hbm = pl.BlockSpec(memory_space=pl.ANY)
    vmem = pl.BlockSpec(memory_space=pltpu.VMEM)
    dens, rest = pl.pallas_call(
        functools.partial(fused_kernel, width_x, width_y, capacity),
        out_shape=(
            pltpu.VMEM((slab_x, slab_y), F32),
            pltpu.VMEM((4, slab_x, slab_y), F32),
        ),
        in_specs=[hbm] * 7,
        out_specs=(vmem, vmem),
        scratch_shapes=[
            pltpu.VMEM((props_count, parcels), F32),
            pltpu.VMEM((1, parcels), jnp.int32),
            pltpu.VMEM((1, parcels), jnp.int32),
            pltpu.VMEM((1, parcels), jnp.int32),
            pltpu.VMEM(class_table.shape, F32),
            pltpu.SMEM(class_table.shape, F32),
            pltpu.VMEM((5, slab_x, slab_y), F32),
            pltpu.VMEM((5, slab_x, slab_y), F32),
            pltpu.VMEM((min(capacity, 256), parcels), BF16),
            pltpu.VMEM((2 * ROWS, parcels), BF16),
            pltpu.VMEM((2 * ROWS, parcels), BF16),
            pltpu.VMEM((2, team, ROWS, capacity), F32),
            pltpu.VMEM((2, team, ROWS, capacity), F32),
            pltpu.VMEM((2 * slab_y, ROWS * capacity), BF16),
            pltpu.VMEM((5, ROWS, capacity), F32),
            pltpu.VMEM((5 * slab_x, 2 * slab_y), BF16),
            pltpu.VMEM((5 * slab_x, 2 * slab_y), F32),
            pltpu.VMEM((5, slab_x, slab_y), F32),
            pltpu.VMEM((5, slab_x, slab_y), F32),
            pltpu.VMEM((2, ROWS, slab_y), F32),
            pltpu.VMEM((2, ROWS, slab_y), F32),
            pltpu.VMEM((2, slab_x, slab_y), F32),
            pltpu.VMEM((2, slab_x, slab_y), F32),
            pltpu.SemaphoreType.DMA((8,)),
            pltpu.SemaphoreType.DMA((2, team)),
            pltpu.SemaphoreType.DMA((2, team)),
            pltpu.SemaphoreType.DMA((2,)),
            pltpu.SemaphoreType.DMA((2,)),
            pltpu.SemaphoreType.DMA((4,)),
            pltpu.SemaphoreType.DMA((4,)),
        ],
        compiler_params=pltpu.CompilerParams(collective_id=0, has_side_effects=True),
    )(
        parcel_props,
        size_class.reshape(1, parcels),
        dest_owner.reshape(1, parcels),
        dest_local.reshape(1, parcels),
        class_table,
        gas_density,
        gas_rest,
    )
    return pl.pallas_call(
        store_kernel,
        out_shape=(
            jax.ShapeDtypeStruct(dens.shape, F32),
            jax.ShapeDtypeStruct(rest.shape, F32),
        ),
        in_specs=[hbm, hbm],
        out_specs=(hbm, hbm),
        scratch_shapes=[pltpu.SemaphoreType.DMA((2,))],
    )(*(pltpu.with_memory_space_constraint(x, pltpu.VMEM) for x in (dens, rest)))


def store_kernel(dens_ref, rest_ref, dens_out, rest_out, sem):
    stores = [
        pltpu.make_async_copy(dens_ref, dens_out, sem.at[0]),
        pltpu.make_async_copy(rest_ref, rest_out, sem.at[1]),
    ]
    for store in stores:
        store.start()
    for store in stores:
        store.wait()


def solution(mesh):
    return jax.shard_map(
        per_device,
        mesh=mesh,
        in_specs=(
            P(None, ("gx", "gy")),
            P(("gx", "gy")),
            P(("gx", "gy"), None),
            P(("gx", "gy")),
            P(),
            P("gx", "gy"),
            P(None, "gx", "gy"),
        ),
        out_specs=(P("gx", "gy"), P(None, "gx", "gy")),
        check_vma=False,
    )
```

time: 34.7 us -> 26.1 us (0.75)
  the two profiles are of different devices: /device:TPU:27 before, /device:TPU:1 now
where the time goes in v1:
time: 26.1 us; the launch traced here: 25.8 us
  Pallas kernels  25.2 us (97%)
  between operations  0.64 us (2%)
    pallas_call x1, Pallas kernels, per_device(): pl.pallas_call(functools.partial(fused_kernel, width_x, width_y, capacity...  24.5 us
    pallas_call x1, Pallas kernels, per_device(): pl.pallas_call(store_kernel, out_shape=(jax.ShapeDtypeStruct(dens.shape,...  0.65 us

profile of v1, /device:TPU:1, one launch (start us, length us, event | category | flops | bytes accessed | tf_op | source)
XLA Modules:
  0.0 25.8 jit_solution(13786977937121757689)
XLA Ops:
  0.6 24.5 %shard_map.86 = (f32[32,128]{1,0:T(8,128)S(1)}, f32[4,32,128]{2,1,0:T(8,128)S(1)}) custom-call(f32[16,4096]{1,0:T(8,128)} %props_hbm.1, s32[1,4096]{1,0:T(1,128)} %bitcast.3, s32[1,4096]{1,0:T(1,128)} %bitcast.4, s32[1,4096]{1,0:T(1,128)} %bitcast.5, f32[8,16]{1,0:T(8,128)} %table_hbm.1, f32[32,128]{1,0:T(8,128)} %dens_hbm.1, f32[4,32,128]{2,1,0:T(8,128)} %rest_hbm.1), custom_call_target="tpu_custom_call" | custom-call | tf_op jit(solution)/shard_map/pallas_call | solution.py:470
  25.2 0.7 %shard_map.87 = (f32[32,128]{1,0:T(8,128)}, f32[4,32,128]{2,1,0:T(8,128)}) custom-call(f32[32,128]{1,0:T(8,128)S(1)} %get-tuple-element.4.dens_ref, f32[4,32,128]{2,1,0:T(8,128)S(1)} %get-tuple-element.5.rest_ref), custom_call_target="tpu_custom_call" | custom-call | tf_op jit(solution)/shard_map/pallas_call | solution.py:520

commit v2 on v1

--- a/solution.py
+++ b/solution.py
@@ -9,9 +9,9 @@
 
 F32 = jnp.float32
 BF16 = jnp.bfloat16
+F8 = jnp.float8_e4m3fn
 LANES = 128
 ROWS = 8
-BATCH = 16
 NT = (((1,), (1,)), ((), ()))
 MESH = pl.DeviceIdType.MESH
 
@@ -21,16 +21,25 @@
     return high, x - high
 
 
+def pick(table, index, axis):
+    other = (1 - axis,)
+    return lax.gather(
+        table,
+        index[..., None],
+        lax.GatherDimensionNumbers(
+            offset_dims=(),
+            collapsed_slice_dims=(axis,),
+            start_index_map=(axis,),
+            operand_batching_dims=other,
+            start_indices_batching_dims=other,
+        ),
+        slice_sizes=(1, 1),
+        mode=lax.GatherScatterMode.PROMISE_IN_BOUNDS,
+    )
+
+
 def iota(shape, dim):
     return lax.broadcasted_iota(jnp.int32, shape, dim)
-
-
-def loop(count, body):
-    if count <= 2:
-        for step in range(count):
-            body(step)
-    else:
-        lax.fori_loop(0, count, lambda step, unused: (body(step), unused)[1], 0)
 
 
 def fused_kernel(
@@ -60,7 +69,6 @@
     packed,
     got,
     spot,
-    gas,
     tab,
     total,
     far_out,
@@ -81,6 +89,8 @@
     deep = width_x // 2
     team = deep * width_y
     groups = team // ROWS
+    tiles = capacity // LANES
+    block = tiles * ROWS
     my_x, my_y = lax.axis_index("gx"), lax.axis_index("gy")
     half = lax.div(my_x, deep)
     row_of = my_x - half * deep
@@ -117,6 +127,12 @@
     def greet(target):
         pl.semaphore_signal(barrier, inc=1, device_id=target, device_id_type=MESH)
 
+    def greet_mate(k, unused):
+        greet(mate(lax.rem(me + k, team)))
+        return unused
+
+    middle = team // 2
+    lax.fori_loop(middle, team, greet_mate, 0, unroll=True if team == 16 else 1)
     greet(mirror)
     last_low = (half == 0) & (row_of == deep - 1)
     first_high = (half == 1) & (row_of == 0)
@@ -129,17 +145,29 @@
     def _():
         greet((my_x - 1, my_y))
 
-    def greet_mate(k, unused):
-        greet(mate(lax.rem(me + k, team)))
-        return unused
-
-    lax.fori_loop(1, team, greet_mate, 0, unroll=5 if team == 16 else 1)
-    border = jnp.where(last_low | first_high, 1, 0)
+    around = [
+        ((mirror[0] + 1, my_y), row_of < deep - 1),
+        ((mirror[0] - 1, my_y), row_of > 0),
+        ((mirror[0], my_y + 1), my_y < width_y - 1),
+        ((mirror[0], my_y - 1), my_y > 0),
+    ]
+    greets = team + jnp.where(last_low | first_high, 1, 0)
+    for target, there in around:
+        greets = greets + jnp.where(there, 1, 0)
+
+        @pl.when(there)
+        def _():
+            greet(target)
+
+    lax.fori_loop(1, middle, greet_mate, 0, unroll=True if team == 16 else 1)
+
+    def rows_of(local):
+        return pl.ds(pl.multiple_of(local * block, ROWS), block)
 
     def copy_to(phase, local):
         return pltpu.make_async_remote_copy(
             src_ref=packed.at[phase, local],
-            dst_ref=got.at[phase, me],
+            dst_ref=got.at[phase, rows_of(me)],
             send_sem=send_sem.at[phase, local],
             recv_sem=recv_sem.at[phase, me],
             device_id=mate(local),
@@ -149,7 +177,7 @@
     def copy_from(phase, local):
         return pltpu.make_async_remote_copy(
             src_ref=packed.at[phase, local],
-            dst_ref=got.at[phase, local],
+            dst_ref=got.at[phase, rows_of(local)],
             send_sem=send_sem.at[phase, local],
             recv_sem=recv_sem.at[phase, local],
             device_id=mate(local),
@@ -194,7 +222,7 @@
                 key = key * spans + level
             at = slice(c * LANES, (c + 1) * LANES)
             keys[:, at] = jnp.broadcast_to(key, (2 * ROWS, LANES)).astype(BF16)
-            hot[:, at] = jnp.where(ranks == rank.astype(BF16), one, zero)
+            hot[:, at] = jnp.where(ranks == rank.astype(BF16), one, zero).astype(F8)
 
     for load in loads[1:]:
         load.wait()
@@ -217,15 +245,13 @@
     mixed = jnp.where(which == 7, cell_ref[...].astype(F32), mixed)
     vals[...] = jnp.concatenate(split(mixed), axis=0).astype(BF16)
 
-    pl.semaphore_wait(barrier, team + border)
-    far_copy(field, far_field, 0).start()
-    batches = team // BATCH
-
-    def send_group(step):
-        phase = step // batches
-        first = (step % batches) * BATCH
-        first_id = jnp.where(phase == half, team, 0) + first
-        count = BATCH * spans // 2
+    def first_of(turn):
+        return lax.rem(lax.div(me, ROWS) + turn, groups) * ROWS
+
+    def pack(phase, turn):
+        first = first_of(turn)
+        first_id = (half * team if phase else (1 - half) * team) + first
+        count = ROWS * spans // 2
         both = [0.0, 0.0]
         for start in range(0, parcels, 256):
             at = slice(start, start + 256)
@@ -246,44 +272,70 @@
                     preferred_element_type=F32,
                 )
         both = jnp.concatenate(both, axis=0)
-        for i in range(BATCH):
+        for i in range(ROWS):
             for k in range(spans):
                 at = 2 * ROWS * (i * spans + k)
-                packed[phase, first + i, :, k * wide : (k + 1) * wide] = (
-                    both[at : at + ROWS] + both[at + ROWS : at + 2 * ROWS]
-                )
-
-        def launch(i, carried):
-            local = first + lax.rem(me + i, BATCH)
-
-            @pl.when(local != me)
-            def _():
-                copy_to(phase, local).start()
-
-            return carried
-
-        lax.fori_loop(1, BATCH + 1, launch, 0, unroll=True)
-
-    loop(2 * batches, send_group)
+                whole = both[at : at + ROWS] + both[at + ROWS : at + 2 * ROWS]
+                for t in range(wide // LANES):
+                    tile = k * (wide // LANES) + t
+                    packed[phase, first + i, tile * ROWS : (tile + 1) * ROWS] = whole[
+                        :, t * LANES : (t + 1) * LANES
+                    ]
+
+    def launch(phase, turn, near):
+        for i in range(1, ROWS if near else ROWS + 1):
+            copy_to(phase, first_of(turn) + lax.rem(me + i, ROWS)).start()
+
+    def send(phase, turn, near):
+        pack(phase, turn)
+        launch(phase, turn, near)
+
+    def send_others(phase, start):
+        if groups - start <= 2:
+            for turn in range(start, groups):
+                send(phase, turn, False)
+        else:
+            lax.fori_loop(start, groups, lambda k, u: (send(phase, k, False), u)[1], 0)
+
+    early = row_of * 2 < deep
+    pack(0, 0)
+    if groups > 1:
+        pack(0, 1)
+    pl.semaphore_wait(barrier, greets)
+
+    @pl.when(early)
+    def _():
+        far_copy(field, far_field, 0).start()
+
+    launch(0, 0, True)
+    if groups > 1:
+        launch(0, 1, False)
+        send_others(0, 2)
+
+    @pl.when(jnp.logical_not(early))
+    def _():
+        far_copy(field, far_field, 0).start()
+
+    send(1, 0, True)
+    send_others(1, 1)
     for phase in range(2):
-        got[phase, me] = packed[phase, me]
+        got[phase, rows_of(me)] = packed[phase, me]
 
     half_x = slab_x // 2
     ys = iota((2 * slab_y, capacity), 0).astype(F32).astype(BF16)
-    xs = iota((half_x, capacity), 0)
-    xs_short = xs.astype(F32).astype(BF16)
-
-    def run_phase(phase, fields):
+    xs_short = iota((half_x, capacity), 0).astype(F32).astype(BF16)
+    sub = iota((ROWS, LANES), 0)
+
+    def prepare(phase, fields):
         parts = []
         for c in range(5):
             for piece in split(fields[c]):
                 parts.append(jnp.concatenate([piece[:half_x], piece[half_x:]], axis=1))
-        tab[...] = jnp.concatenate(parts, axis=0).astype(BF16)
-        total[...] = jnp.zeros_like(total)
-
-        def take_group(step, unused):
-            turn = lax.div(me, ROWS) + step
-            first = lax.rem(turn, groups) * ROWS
+        tab[phase] = jnp.concatenate(parts, axis=0).astype(BF16)
+
+    def take_group(phase, turn):
+        if True:
+            first = first_of(turn)
 
             def arrive(i, carried):
                 @pl.when(first + i != me)
@@ -296,28 +348,48 @@
 
             def part(c):
                 return jnp.concatenate(
-                    [got[phase, first + i][c : c + 1] for i in range(ROWS)], axis=0
+                    [
+                        got[phase, pl.ds(first * block + t * ROWS + c, ROWS, stride=block), :]
+                        for t in range(tiles)
+                    ],
+                    axis=1,
                 )
 
             cell = part(7).astype(jnp.int32)
             line = lax.div(cell, slab_y)
+            lane_of = cell - line * slab_y
             upper_half = jnp.where(line >= half_x, 1, 0)
-            lanes_at = (cell - line * slab_y + upper_half * slab_y).astype(F32)
-            lines_at = line - upper_half * half_x
-            lines_short = lines_at.astype(F32)
+            lanes_at = (lane_of + upper_half * slab_y).astype(F32)
+            lines_short = (line - upper_half * half_x).astype(F32)
+            line_at = line - upper_half * half_x
+            shelf = lax.div(line_at, ROWS)
+            within = line_at - shelf * ROWS
+            gas = [[jnp.zeros((ROWS, LANES), F32)] * tiles for c in range(5)]
             for i in range(ROWS):
                 spot_at = slice(i * capacity, (i + 1) * capacity)
                 spot[:, spot_at] = jnp.where(
                     ys == lanes_at[i : i + 1].astype(BF16), one, zero
-                )
-                found = jnp.dot(tab[...], spot[:, spot_at], preferred_element_type=F32)
-                in_row = xs == lines_at[i : i + 1]
-                for c in range(5):
-                    at = 2 * c * half_x
-                    both = found[at : at + half_x] + found[at + half_x : at + 2 * half_x]
-                    gas[c, i : i + 1] = jnp.sum(
-                        jnp.where(in_row, both, 0.0), axis=0, keepdims=True
-                    )
+                ).astype(F8)
+                found = jnp.dot(tab[phase], spot[:, spot_at], preferred_element_type=F32)
+                for t in range(tiles):
+                    lanes = slice(t * LANES, (t + 1) * LANES)
+                    low, deep_row = [
+                        jnp.broadcast_to(x[i : i + 1, lanes], (ROWS, LANES))
+                        for x in (within, shelf)
+                    ]
+                    for c in range(5):
+                        pieces = []
+                        for p in range(2):
+                            at = (2 * c + p) * half_x
+                            piece = found[at : at + ROWS, lanes]
+                            for r in range(1, half_x // ROWS):
+                                here = found[at + r * ROWS : at + (r + 1) * ROWS, lanes]
+                                piece = jnp.where(deep_row >= r, here, piece)
+                            pieces.append(piece)
+                        gas[c][t] = jnp.where(
+                            sub == i, pick(pieces[0] + pieces[1], low, 0), gas[c][t]
+                        )
+            gas = [jnp.concatenate(row, axis=1) for row in gas]
 
             kind = part(6).astype(jnp.int32)
             coefs = [jnp.full(kind.shape, scalars_ref[0, j], F32) for j in range(5)]
@@ -351,72 +423,104 @@
                         axis=0,
                     )
                 )
-            part_total = 0.0
-            for at in (0, ROWS // 2):
-                part_total += lax.dot_general(
+            for side in range(2):
+                at = side * ROWS // 2
+                total[phase, side] += lax.dot_general(
                     jnp.concatenate(spread[at : at + ROWS // 2], axis=1),
                     spot[:, at * capacity : (at + ROWS // 2) * capacity],
                     NT,
                     preferred_element_type=F32,
                 )
-            total[...] += part_total
-            return unused
-
-        lax.fori_loop(0, groups, take_group, 0)
+
+    def deposit_of(phase):
+        whole = total[phase, 0] + total[phase, 1]
         summed = []
         for c in range(5):
             at = 2 * c * half_x
-            both = total[at : at + half_x] + total[at + half_x : at + 2 * half_x]
+            both = whole[at : at + half_x] + whole[at + half_x : at + 2 * half_x]
             summed.append(jnp.concatenate([both[:, :slab_y], both[:, slab_y:]], axis=0))
         return summed
 
-    far_copy(field, far_field, 0).wait_recv()
-    for c, piece in enumerate(run_phase(0, far_field)):
-        far_out[c] = piece
-    far_copy(far_out, far_in, 1).start()
-    mine = run_phase(1, field)
-    far_copy(far_out, far_in, 1).wait_recv()
-    deposit = [mine[c] + far_in[c] for c in range(5)]
     lane = iota((slab_x, slab_y), 1)
-    low_edge = jnp.zeros((slab_x, slab_y), F32)
-    high_edge = jnp.zeros((slab_x, slab_y), F32)
-    row_out[...] = jnp.zeros_like(row_out)
-    for c in range(5):
-        row_out[0, c : c + 1] = deposit[c][0:1]
-        row_out[1, c : c + 1] = deposit[c][slab_x - 1 : slab_x]
-        low_edge = jnp.where(
-            lane == c, pltpu.roll(deposit[c], c, 1) if c else deposit[c], low_edge
-        )
-        high_edge = jnp.where(lane == c, pltpu.roll(deposit[c], c + 1, 1), high_edge)
-    col_out[0] = low_edge
-    col_out[1] = high_edge
-
-    def edge(out_ref, in_ref, side, base, target):
+
+    def edges_of(origin):
+        x, y = origin
+        return [
+            (row_out, row_in, 0, 0, (x - 1, y), x > 0, my_x < width_x - 1),
+            (row_out, row_in, 1, 0, (x + 1, y), x < width_x - 1, my_x > 0),
+            (col_out, col_in, 0, 2, (x, y - 1), y > 0, my_y < width_y - 1),
+            (col_out, col_in, 1, 2, (x, y + 1), y < width_y - 1, my_y > 0),
+        ]
+
+    def edge(phase, out_ref, in_ref, side, base, target):
+        at = 4 * phase + base + side
         return pltpu.make_async_remote_copy(
-            src_ref=out_ref.at[side],
-            dst_ref=in_ref.at[side],
-            send_sem=halo_send.at[base + side],
-            recv_sem=halo_recv.at[base + side],
+            src_ref=out_ref.at[phase, side],
+            dst_ref=in_ref.at[phase, side],
+            send_sem=halo_send.at[at],
+            recv_sem=halo_recv.at[at],
             device_id=target,
             device_id_type=MESH,
         )
 
-    edges = [
-        (row_out, row_in, 0, 0, (my_x - 1, my_y), my_x > 0, my_x < width_x - 1),
-        (row_out, row_in, 1, 0, (my_x + 1, my_y), my_x < width_x - 1, my_x > 0),
-        (col_out, col_in, 0, 2, (my_x, my_y - 1), my_y > 0, my_y < width_y - 1),
-        (col_out, col_in, 1, 2, (my_x, my_y + 1), my_y < width_y - 1, my_y > 0),
-    ]
-    for out_ref, in_ref, side, base, target, sends, takes in edges:
-
-        @pl.when(sends)
-        def _(out_ref=out_ref, in_ref=in_ref, side=side, base=base, target=target):
-            edge(out_ref, in_ref, side, base, target).start()
+    origins = (mirror, (my_x, my_y))
+
+    def send_edges(phase, deposit):
+        sides = jnp.zeros((slab_x, slab_y), F32)
+        for c in range(5):
+            row_out[phase, 0, c : c + 1] = deposit[c][0:1]
+            row_out[phase, 1, c : c + 1] = deposit[c][slab_x - 1 : slab_x]
+            first = pltpu.roll(deposit[c], c, 1) if c else deposit[c]
+            sides = jnp.where(lane == c, first, sides)
+            last = pltpu.roll(deposit[c], ROWS + c + 1, 1)
+            sides = jnp.where(lane == ROWS + c, last, sides)
+        turned = jnp.transpose(sides)
+        for side in range(2):
+            col_out[phase, side, :, :slab_x] = turned[side * ROWS : (side + 1) * ROWS]
+        for out_ref, in_ref, side, base, target, sends, takes in edges_of(origins[phase]):
+
+            @pl.when(sends)
+            def _():
+                edge(phase, out_ref, in_ref, side, base, target).start()
+
+    for ref in (row_out, col_out):
+        ref[...] = jnp.zeros_like(ref)
+    for out_ref, in_ref, side, base, target, sends, takes in edges_of(origins[1]):
 
         @pl.when(jnp.logical_not(takes))
-        def _(in_ref=in_ref, side=side):
-            in_ref[side] = jnp.zeros(in_ref.shape[1:], F32)
-
+        def _():
+            for phase in range(2):
+                in_ref[phase, side] = jnp.zeros(in_ref.shape[2:], F32)
+
+    total[...] = jnp.zeros_like(total)
+    prepare(1, field)
+    lead = jnp.where(early, 0, 1)
+
+    def step(t, unused):
+        at = t - lead
+
+        @pl.when(at == 0)
+        def _():
+            far_copy(field, far_field, 0).wait_recv()
+            prepare(0, far_field)
+
+        far_turn = (at >= 0) & (at < groups)
+        phase = jnp.where(far_turn, 0, 1)
+        take_group(phase, jnp.where(far_turn, at, jnp.where(at < 0, 0, t - groups)))
+
+        @pl.when(at == groups - 1)
+        def _():
+            deposit = deposit_of(0)
+            for c in range(5):
+                far_out[c] = deposit[c]
+            send_edges(0, deposit)
+            far_copy(far_out, far_in, 1).start()
+
+        return unused
+
+    lax.fori_loop(0, 2 * groups, step, 0)
+    mine = deposit_of(1)
+    send_edges(1, mine)
     def wait_sent(k, unused):
         local = lax.rem(me + k, team)
         for phase in range(2):
@@ -426,34 +530,37 @@
     lax.fori_loop(1, team, wait_sent, 0)
     far_copy(field, far_field, 0).wait_send()
     far_copy(far_out, far_in, 1).wait_send()
-    for out_ref, in_ref, side, base, target, sends, takes in edges:
-
-        @pl.when(takes)
-        def _(out_ref=out_ref, in_ref=in_ref, side=side, base=base, target=target):
-            edge(out_ref, in_ref, side, base, target).wait_recv()
-
+    far_copy(far_out, far_in, 1).wait_recv()
+    for phase in range(2):
+        for out_ref, in_ref, side, base, target, sends, takes in edges_of(origins[1]):
+
+            @pl.when(takes)
+            def _():
+                edge(phase, out_ref, in_ref, side, base, target).wait_recv()
+
+    rows_in = [row_in[0, side] + row_in[1, side] for side in range(2)]
+    cols_in = [
+        jnp.transpose(col_in[0, side] + col_in[1, side])[:slab_x] for side in range(2)
+    ]
     for c in range(5):
-        here = deposit[c]
-        above = jnp.concatenate([row_in[1, c : c + 1], here[: slab_x - 1]], axis=0)
-        below = jnp.concatenate([here[1:], row_in[0, c : c + 1]], axis=0)
-        left_in = pltpu.roll(col_in[1], slab_y - c, 1) if c else col_in[1]
-        left = jnp.where(lane == 0, left_in, pltpu.roll(here, 1, 1))
-        right = jnp.where(
-            lane == slab_y - 1,
-            pltpu.roll(col_in[0], slab_y - 1 - c, 1),
-            pltpu.roll(here, slab_y - 1, 1),
-        )
+        here = mine[c] + far_in[c]
+        above = jnp.concatenate([rows_in[1][c : c + 1], here[: slab_x - 1]], axis=0)
+        below = jnp.concatenate([here[1:], rows_in[0][c : c + 1]], axis=0)
+        beside = [jnp.broadcast_to(x[:, c : c + 1], (slab_x, slab_y)) for x in cols_in]
+        left = jnp.where(lane == 0, beside[1], pltpu.roll(here, 1, 1))
+        right = jnp.where(lane == slab_y - 1, beside[0], pltpu.roll(here, slab_y - 1, 1))
         smooth = 0.4 * here + 0.15 * (below + above + right + left)
         if c:
             rest_out[c - 1] = field[c] + smooth
         else:
             dens_out[...] = field[0] + smooth
 
-    for out_ref, in_ref, side, base, target, sends, takes in edges:
-
-        @pl.when(sends)
-        def _(out_ref=out_ref, in_ref=in_ref, side=side, base=base, target=target):
-            edge(out_ref, in_ref, side, base, target).wait_send()
+    for phase in range(2):
+        for out_ref, in_ref, side, base, target, sends, takes in edges_of(origins[phase]):
+
+            @pl.when(sends)
+            def _():
+                edge(phase, out_ref, in_ref, side, base, target).wait_send()
 
 
 def per_device(
@@ -484,28 +591,27 @@
             pltpu.SMEM(class_table.shape, F32),
             pltpu.VMEM((5, slab_x, slab_y), F32),
             pltpu.VMEM((5, slab_x, slab_y), F32),
-            pltpu.VMEM((min(capacity, 256), parcels), BF16),
+            pltpu.VMEM((min(capacity, 256), parcels), F8),
             pltpu.VMEM((2 * ROWS, parcels), BF16),
             pltpu.VMEM((2 * ROWS, parcels), BF16),
-            pltpu.VMEM((2, team, ROWS, capacity), F32),
-            pltpu.VMEM((2, team, ROWS, capacity), F32),
-            pltpu.VMEM((2 * slab_y, ROWS * capacity), BF16),
-            pltpu.VMEM((5, ROWS, capacity), F32),
-            pltpu.VMEM((5 * slab_x, 2 * slab_y), BF16),
-            pltpu.VMEM((5 * slab_x, 2 * slab_y), F32),
+            pltpu.VMEM((2, team, capacity // LANES * ROWS, LANES), F32),
+            pltpu.VMEM((2, team * capacity // LANES * ROWS, LANES), F32),
+            pltpu.VMEM((2 * slab_y, ROWS * capacity), F8),
+            pltpu.VMEM((2, 5 * slab_x, 2 * slab_y), BF16),
+            pltpu.VMEM((2, 2, 5 * slab_x, 2 * slab_y), F32),
             pltpu.VMEM((5, slab_x, slab_y), F32),
             pltpu.VMEM((5, slab_x, slab_y), F32),
-            pltpu.VMEM((2, ROWS, slab_y), F32),
-            pltpu.VMEM((2, ROWS, slab_y), F32),
-            pltpu.VMEM((2, slab_x, slab_y), F32),
-            pltpu.VMEM((2, slab_x, slab_y), F32),
+            pltpu.VMEM((2, 2, ROWS, slab_y), F32),
+            pltpu.VMEM((2, 2, ROWS, slab_y), F32),
+            pltpu.VMEM((2, 2, ROWS, LANES), F32),
+            pltpu.VMEM((2, 2, ROWS, LANES), F32),
             pltpu.SemaphoreType.DMA((8,)),
             pltpu.SemaphoreType.DMA((2, team)),
             pltpu.SemaphoreType.DMA((2, team)),
             pltpu.SemaphoreType.DMA((2,)),
             pltpu.SemaphoreType.DMA((2,)),
-            pltpu.SemaphoreType.DMA((4,)),
-            pltpu.SemaphoreType.DMA((4,)),
+            pltpu.SemaphoreType.DMA((8,)),
+            pltpu.SemaphoreType.DMA((8,)),
         ],
         compiler_params=pltpu.CompilerParams(collective_id=0, has_side_effects=True),
     )(

time: 26.1 us -> 21.7 us (0.83)
  the two profiles are of different devices: /device:TPU:1 before, /device:TPU:0 now
where the time goes in v2:
time: 21.7 us; the launch traced here: 21.5 us
  Pallas kernels  20.8 us (96%)
  between operations  0.64 us (3%)
    pallas_call x1, Pallas kernels, per_device(): pl.pallas_call(functools.partial(fused_kernel, width_x, width_y, capacity...  20.2 us
    pallas_call x1, Pallas kernels, per_device(): pl.pallas_call(store_kernel, out_shape=(jax.ShapeDtypeStruct(dens.shape,...  0.65 us

profile of v2, /device:TPU:0, one launch (start us, length us, event | category | flops | bytes accessed | tf_op | source)
XLA Modules:
  0.0 21.5 jit_solution(15901593212091238061)
XLA Ops:
  0.6 20.2 %shard_map.86 = (f32[32,128]{1,0:T(8,128)S(1)}, f32[4,32,128]{2,1,0:T(8,128)S(1)}) custom-call(f32[16,4096]{1,0:T(8,128)} %props_hbm.1, s32[1,4096]{1,0:T(1,128)} %bitcast.3, s32[1,4096]{1,0:T(1,128)} %bitcast.4, s32[1,4096]{1,0:T(1,128)} %bitcast.5, f32[8,16]{1,0:T(8,128)} %table_hbm.1, f32[32,128]{1,0:T(8,128)} %dens_hbm.1, f32[4,32,128]{2,1,0:T(8,128)} %rest_hbm.1), custom_call_target="tpu_custom_call" | custom-call | tf_op jit(solution)/shard_map/pallas_call | solution.py:577
  20.8 0.7 %shard_map.87 = (f32[32,128]{1,0:T(8,128)}, f32[4,32,128]{2,1,0:T(8,128)}) custom-call(f32[32,128]{1,0:T(8,128)S(1)} %get-tuple-element.4.dens_ref, f32[4,32,128]{2,1,0:T(8,128)S(1)} %get-tuple-element.5.rest_ref), custom_call_target="tpu_custom_call" | custom-call | tf_op jit(solution)/shard_map/pallas_call | solution.py:626

commit v3 on v2

--- a/solution.py
+++ b/solution.py
@@ -62,7 +62,8 @@
     table_ref,
     scalars_ref,
     field,
-    far_field,
+    flow,
+    far_flow,
     hot,
     vals,
     keys,
@@ -82,7 +83,6 @@
     recv_sem,
     far_send,
     far_recv,
-    halo_send,
     halo_recv,
 ):
     devices = width_x * width_y
@@ -168,21 +168,22 @@
         return pltpu.make_async_remote_copy(
             src_ref=packed.at[phase, local],
             dst_ref=got.at[phase, rows_of(me)],
-            send_sem=send_sem.at[phase, local],
-            recv_sem=recv_sem.at[phase, me],
+            send_sem=send_sem.at[phase],
+            recv_sem=recv_sem.at[phase, lax.div(me, ROWS)],
             device_id=mate(local),
             device_id_type=MESH,
         )
 
-    def copy_from(phase, local):
-        return pltpu.make_async_remote_copy(
-            src_ref=packed.at[phase, local],
-            dst_ref=got.at[phase, rows_of(local)],
-            send_sem=send_sem.at[phase, local],
-            recv_sem=recv_sem.at[phase, local],
-            device_id=mate(local),
+    def wait_blocks(phase, first, count):
+        blocks = got.at[phase, pl.ds(pl.multiple_of(first * block, ROWS), count * block)]
+        pltpu.make_async_remote_copy(
+            src_ref=blocks,
+            dst_ref=blocks,
+            send_sem=send_sem.at[phase],
+            recv_sem=recv_sem.at[phase, lax.div(first, ROWS)],
+            device_id=mirror,
             device_id_type=MESH,
-        )
+        ).wait_recv()
 
     def far_copy(out_ref, in_ref, i):
         return pltpu.make_async_remote_copy(
@@ -226,6 +227,9 @@
 
     for load in loads[1:]:
         load.wait()
+    inverse = 1.0 / field[0]
+    for c in range(4):
+        flow[c] = field[c + 1] * inverse
     eye = jnp.where(
         iota((props_count, props_count), 0) == iota((props_count, props_count), 1), 1.0, 0.0
     ).astype(BF16)
@@ -305,7 +309,7 @@
 
     @pl.when(early)
     def _():
-        far_copy(field, far_field, 0).start()
+        far_copy(flow, far_flow, 0).start()
 
     launch(0, 0, True)
     if groups > 1:
@@ -314,7 +318,7 @@
 
     @pl.when(jnp.logical_not(early))
     def _():
-        far_copy(field, far_field, 0).start()
+        far_copy(flow, far_flow, 0).start()
 
     send(1, 0, True)
     send_others(1, 1)
@@ -328,7 +332,7 @@
 
     def prepare(phase, fields):
         parts = []
-        for c in range(5):
+        for c in range(4):
             for piece in split(fields[c]):
                 parts.append(jnp.concatenate([piece[:half_x], piece[half_x:]], axis=1))
         tab[phase] = jnp.concatenate(parts, axis=0).astype(BF16)
@@ -337,14 +341,13 @@
         if True:
             first = first_of(turn)
 
-            def arrive(i, carried):
-                @pl.when(first + i != me)
-                def _():
-                    copy_from(phase, first + i).wait_recv()
-
-                return carried
-
-            lax.fori_loop(0, ROWS, arrive, 0, unroll=True)
+            @pl.when(turn == 0)
+            def _():
+                wait_blocks(phase, first, ROWS - 1)
+
+            @pl.when(turn != 0)
+            def _():
+                wait_blocks(phase, first, ROWS)
 
             def part(c):
                 return jnp.concatenate(
@@ -364,7 +367,7 @@
             line_at = line - upper_half * half_x
             shelf = lax.div(line_at, ROWS)
             within = line_at - shelf * ROWS
-            gas = [[jnp.zeros((ROWS, LANES), F32)] * tiles for c in range(5)]
+            gas = [[jnp.zeros((ROWS, LANES), F32)] * tiles for c in range(4)]
             for i in range(ROWS):
                 spot_at = slice(i * capacity, (i + 1) * capacity)
                 spot[:, spot_at] = jnp.where(
@@ -377,7 +380,7 @@
                         jnp.broadcast_to(x[i : i + 1, lanes], (ROWS, LANES))
                         for x in (within, shelf)
                     ]
-                    for c in range(5):
+                    for c in range(4):
                         pieces = []
                         for p in range(2):
                             at = (2 * c + p) * half_x
@@ -399,9 +402,8 @@
             mass = part(0)
             speed = [part(j) for j in (1, 2, 3)]
             heat, energy = part(4), part(5)
-            inverse = 1.0 / gas[0]
-            slip = [speed[j] - gas[j + 1] * inverse for j in range(3)]
-            excess = heat - gas[4] * inverse
+            slip = [speed[j] - gas[j] for j in range(3)]
+            excess = heat - gas[3]
             soft = jnp.maximum(excess, 0.0) + jnp.log1p(jnp.exp(-jnp.abs(excess)))
             evapor = mass * (1.0 - jnp.exp(-(coefs[0] * soft)))
             square = slip[0] * slip[0] + slip[1] * slip[1] + slip[2] * slip[2]
@@ -457,7 +459,7 @@
         return pltpu.make_async_remote_copy(
             src_ref=out_ref.at[phase, side],
             dst_ref=in_ref.at[phase, side],
-            send_sem=halo_send.at[at],
+            send_sem=load_sem.at[at],
             recv_sem=halo_recv.at[at],
             device_id=target,
             device_id_type=MESH,
@@ -493,27 +495,35 @@
                 in_ref[phase, side] = jnp.zeros(in_ref.shape[2:], F32)
 
     total[...] = jnp.zeros_like(total)
-    prepare(1, field)
-    lead = jnp.where(early, 0, 1)
+    prepare(1, flow)
+    own_first = (half == 0) & jnp.logical_not(early)
+    lead = jnp.where(own_first if groups == 1 else half == 0, 1, 0)
+
+    hold = jnp.where((half == 1) & jnp.logical_not(early), min(groups, 2), 0)
 
     def step(t, unused):
-        at = t - lead
-
-        @pl.when(at == 0)
+        head = (lead == 1) & (t < 2)
+        far_turn = jnp.where(
+            head, jnp.where(own_first, t, 1 - t), jnp.where(t < groups + lead, 1, 0)
+        )
+        turn = jnp.where(head, 0, jnp.where(far_turn == 1, t - lead, t - groups))
+
+        @pl.when(t == jnp.where(own_first, 1, 0))
         def _():
-            far_copy(field, far_field, 0).wait_recv()
-            prepare(0, far_field)
-
-        far_turn = (at >= 0) & (at < groups)
-        phase = jnp.where(far_turn, 0, 1)
-        take_group(phase, jnp.where(far_turn, at, jnp.where(at < 0, 0, t - groups)))
-
-        @pl.when(at == groups - 1)
+            far_copy(flow, far_flow, 0).wait_recv()
+            prepare(0, far_flow)
+
+        take_group(1 - far_turn, turn)
+
+        @pl.when(t == groups - 1 + lead)
         def _():
             deposit = deposit_of(0)
             for c in range(5):
                 far_out[c] = deposit[c]
             send_edges(0, deposit)
+
+        @pl.when(t == groups - 1 + lead + hold)
+        def _():
             far_copy(far_out, far_in, 1).start()
 
         return unused
@@ -521,14 +531,17 @@
     lax.fori_loop(0, 2 * groups, step, 0)
     mine = deposit_of(1)
     send_edges(1, mine)
-    def wait_sent(k, unused):
-        local = lax.rem(me + k, team)
-        for phase in range(2):
-            copy_to(phase, local).wait_send()
-        return unused
-
-    lax.fori_loop(1, team, wait_sent, 0)
-    far_copy(field, far_field, 0).wait_send()
+    for phase in range(2):
+        blocks = packed.at[phase, pl.ds(0, team - 1)]
+        pltpu.make_async_remote_copy(
+            src_ref=blocks,
+            dst_ref=blocks,
+            send_sem=send_sem.at[phase],
+            recv_sem=recv_sem.at[phase, 0],
+            device_id=mirror,
+            device_id_type=MESH,
+        ).wait_send()
+    far_copy(flow, far_flow, 0).wait_send()
     far_copy(far_out, far_in, 1).wait_send()
     far_copy(far_out, far_in, 1).wait_recv()
     for phase in range(2):
@@ -590,14 +603,15 @@
             pltpu.VMEM(class_table.shape, F32),
             pltpu.SMEM(class_table.shape, F32),
             pltpu.VMEM((5, slab_x, slab_y), F32),
-            pltpu.VMEM((5, slab_x, slab_y), F32),
+            pltpu.VMEM((4, slab_x, slab_y), F32),
+            pltpu.VMEM((4, slab_x, slab_y), F32),
             pltpu.VMEM((min(capacity, 256), parcels), F8),
             pltpu.VMEM((2 * ROWS, parcels), BF16),
             pltpu.VMEM((2 * ROWS, parcels), BF16),
             pltpu.VMEM((2, team, capacity // LANES * ROWS, LANES), F32),
             pltpu.VMEM((2, team * capacity // LANES * ROWS, LANES), F32),
             pltpu.VMEM((2 * slab_y, ROWS * capacity), F8),
-            pltpu.VMEM((2, 5 * slab_x, 2 * slab_y), BF16),
+            pltpu.VMEM((2, 4 * slab_x, 2 * slab_y), BF16),
             pltpu.VMEM((2, 2, 5 * slab_x, 2 * slab_y), F32),
             pltpu.VMEM((5, slab_x, slab_y), F32),
             pltpu.VMEM((5, slab_x, slab_y), F32),
@@ -606,11 +620,10 @@
             pltpu.VMEM((2, 2, ROWS, LANES), F32),
             pltpu.VMEM((2, 2, ROWS, LANES), F32),
             pltpu.SemaphoreType.DMA((8,)),
-            pltpu.SemaphoreType.DMA((2, team)),
-            pltpu.SemaphoreType.DMA((2, team)),
+            pltpu.SemaphoreType.DMA((2,)),
+            pltpu.SemaphoreType.DMA((2, team // ROWS)),
             pltpu.SemaphoreType.DMA((2,)),
             pltpu.SemaphoreType.DMA((2,)),
-            pltpu.SemaphoreType.DMA((8,)),
             pltpu.SemaphoreType.DMA((8,)),
         ],
         compiler_params=pltpu.CompilerParams(collective_id=0, has_side_effects=True),

time: 21.7 us -> 20.7 us (0.954)
  Pallas kernels: 20.8 us -> 19.8 us
    pallas_call x1, Pallas kernels: 20.2 us -> 19.2 us  [per_device(): pl.pallas_call(functools.partial(fused_kernel, width_x, width_y, capacity...]
where the time goes in v3:
time: 20.7 us; the launch traced here: 20.4 us
  Pallas kernels  19.8 us (96%)
  between operations  0.64 us (3%)
    pallas_call x1, Pallas kernels, per_device(): pl.pallas_call(functools.partial(fused_kernel, width_x, width_y, capacity...  19.2 us
    pallas_call x1, Pallas kernels, per_device(): pl.pallas_call(store_kernel, out_shape=(jax.ShapeDtypeStruct(dens.shape,...  0.65 us

profile of v3, /device:TPU:0, one launch (start us, length us, event | category | flops | bytes accessed | tf_op | source)
XLA Modules:
  0.0 20.4 jit_solution(16619389136074035760)
XLA Ops:
  0.6 19.2 %shard_map.86 = (f32[32,128]{1,0:T(8,128)S(1)}, f32[4,32,128]{2,1,0:T(8,128)S(1)}) custom-call(f32[16,4096]{1,0:T(8,128)} %props_hbm.1, s32[1,4096]{1,0:T(1,128)} %bitcast.3, s32[1,4096]{1,0:T(1,128)} %bitcast.4, s32[1,4096]{1,0:T(1,128)} %bitcast.5, f32[8,16]{1,0:T(8,128)} %table_hbm.1, f32[32,128]{1,0:T(8,128)} %dens_hbm.1, f32[4,32,128]{2,1,0:T(8,128)} %rest_hbm.1), custom_call_target="tpu_custom_call" | custom-call | tf_op jit(solution)/shard_map/pallas_call | solution.py:590
  19.8 0.7 %shard_map.87 = (f32[32,128]{1,0:T(8,128)}, f32[4,32,128]{2,1,0:T(8,128)}) custom-call(f32[32,128]{1,0:T(8,128)S(1)} %get-tuple-element.4.dens_ref, f32[4,32,128]{2,1,0:T(8,128)S(1)} %get-tuple-element.5.rest_ref), custom_call_target="tpu_custom_call" | custom-call | tf_op jit(solution)/shard_map/pallas_call | solution.py:639

commit v4 on v3

--- a/solution.py
+++ b/solution.py
@@ -254,7 +254,7 @@
 
     def pack(phase, turn):
         first = first_of(turn)
-        first_id = (half * team if phase else (1 - half) * team) + first
+        first_id = jnp.where(phase == half, team, 0) + first
         count = ROWS * spans // 2
         both = [0.0, 0.0]
         for start in range(0, parcels, 256):
@@ -302,26 +302,37 @@
             lax.fori_loop(start, groups, lambda k, u: (send(phase, k, False), u)[1], 0)
 
     early = row_of * 2 < deep
-    pack(0, 0)
+    low = jnp.where(half == 0, 1, 0)
+    low_inner = jnp.where((half == 0) & jnp.logical_not(early), 1, 0)
+    low_outer = low - low_inner
+    pack(low_inner, 0)
     if groups > 1:
-        pack(0, 1)
+        pack(low_outer, 1)
     pl.semaphore_wait(barrier, greets)
 
     @pl.when(early)
     def _():
         far_copy(flow, far_flow, 0).start()
 
-    launch(0, 0, True)
+    launch(low_inner, 0, True)
     if groups > 1:
-        launch(0, 1, False)
-        send_others(0, 2)
+        launch(low_outer, 1, False)
+        send_others(low_outer, 2)
 
     @pl.when(jnp.logical_not(early))
     def _():
         far_copy(flow, far_flow, 0).start()
 
-    send(1, 0, True)
-    send_others(1, 1)
+    @pl.when(low_outer == 1)
+    def _():
+        send(1, 0, True)
+        send_others(0, 1)
+
+    @pl.when(low_outer == 0)
+    def _():
+        send_others(1, 1)
+        send(1 - low_inner, 0, True)
+
     for phase in range(2):
         got[phase, rows_of(me)] = packed[phase, me]
 
@@ -496,33 +507,39 @@
 
     total[...] = jnp.zeros_like(total)
     prepare(1, flow)
-    own_first = (half == 0) & jnp.logical_not(early)
-    lead = jnp.where(own_first if groups == 1 else half == 0, 1, 0)
+    far_start = low_inner * groups
+    far_stop = groups - 1 + low_outer + low_inner * groups
+    own_stop = 2 * groups - 1 - low_inner * groups
+    if groups == 1:
+        far_stop, own_stop = low_inner, 1 - low_inner
 
     hold = jnp.where((half == 1) & jnp.logical_not(early), min(groups, 2), 0)
 
     def step(t, unused):
-        head = (lead == 1) & (t < 2)
-        far_turn = jnp.where(
-            head, jnp.where(own_first, t, 1 - t), jnp.where(t < groups + lead, 1, 0)
-        )
-        turn = jnp.where(head, 0, jnp.where(far_turn == 1, t - lead, t - groups))
-
-        @pl.when(t == jnp.where(own_first, 1, 0))
+        head = (low_outer == 1) & (t < 2)
+        ahead = jnp.where(t < groups + low_outer, 1, 0)
+        far_turn = jnp.where(head, 1 - t, jnp.where(low_inner == 1, 1 - ahead, ahead))
+        turn = jnp.where(head, 0, jnp.where(ahead == 1, t - low_outer, t - groups))
+
+        @pl.when(t == far_start)
         def _():
             far_copy(flow, far_flow, 0).wait_recv()
             prepare(0, far_flow)
 
         take_group(1 - far_turn, turn)
 
-        @pl.when(t == groups - 1 + lead)
+        @pl.when(t == far_stop)
         def _():
             deposit = deposit_of(0)
             for c in range(5):
                 far_out[c] = deposit[c]
             send_edges(0, deposit)
 
-        @pl.when(t == groups - 1 + lead + hold)
+        @pl.when(t == own_stop)
+        def _():
+            send_edges(1, deposit_of(1))
+
+        @pl.when(t == far_stop + hold)
         def _():
             far_copy(far_out, far_in, 1).start()
 
@@ -530,19 +547,6 @@
 
     lax.fori_loop(0, 2 * groups, step, 0)
     mine = deposit_of(1)
-    send_edges(1, mine)
-    for phase in range(2):
-        blocks = packed.at[phase, pl.ds(0, team - 1)]
-        pltpu.make_async_remote_copy(
-            src_ref=blocks,
-            dst_ref=blocks,
-            send_sem=send_sem.at[phase],
-            recv_sem=recv_sem.at[phase, 0],
-            device_id=mirror,
-            device_id_type=MESH,
-        ).wait_send()
-    far_copy(flow, far_flow, 0).wait_send()
-    far_copy(far_out, far_in, 1).wait_send()
     far_copy(far_out, far_in, 1).wait_recv()
     for phase in range(2):
         for out_ref, in_ref, side, base, target, sends, takes in edges_of(origins[1]):
@@ -568,6 +572,18 @@
         else:
             dens_out[...] = field[0] + smooth
 
+    for phase in range(2):
+        blocks = packed.at[phase, pl.ds(0, team - 1)]
+        pltpu.make_async_remote_copy(
+            src_ref=blocks,
+            dst_ref=blocks,
+            send_sem=send_sem.at[phase],
+            recv_sem=recv_sem.at[phase, 0],
+            device_id=mirror,
+            device_id_type=MESH,
+        ).wait_send()
+    far_copy(flow, far_flow, 0).wait_send()
+    far_copy(far_out, far_in, 1).wait_send()
     for phase in range(2):
         for out_ref, in_ref, side, base, target, sends, takes in edges_of(origins[phase]):
 

time: 20.7 us -> 20.7 us (level)
  no operation moved by 1% of the time
where the time goes in v4:
time: 20.7 us; the launch traced here: 20.5 us
  Pallas kernels  19.8 us (96%)
  between operations  0.64 us (3%)
    pallas_call x1, Pallas kernels, per_device(): pl.pallas_call(functools.partial(fused_kernel, width_x, width_y, capacity...  19.2 us
    pallas_call x1, Pallas kernels, per_device(): pl.pallas_call(store_kernel, out_shape=(jax.ShapeDtypeStruct(dens.shape,...  0.65 us

profile of v4, /device:TPU:0, one launch (start us, length us, event | category | flops | bytes accessed | tf_op | source)
XLA Modules:
  0.0 20.5 jit_solution(3094353012293729744)
XLA Ops:
  0.6 19.2 %shard_map.86 = (f32[32,128]{1,0:T(8,128)S(1)}, f32[4,32,128]{2,1,0:T(8,128)S(1)}) custom-call(f32[16,4096]{1,0:T(8,128)} %props_hbm.1, s32[1,4096]{1,0:T(1,128)} %bitcast.3, s32[1,4096]{1,0:T(1,128)} %bitcast.4, s32[1,4096]{1,0:T(1,128)} %bitcast.5, f32[8,16]{1,0:T(8,128)} %table_hbm.1, f32[32,128]{1,0:T(8,128)} %dens_hbm.1, f32[4,32,128]{2,1,0:T(8,128)} %rest_hbm.1), custom_call_target="tpu_custom_call" | custom-call | tf_op jit(solution)/shard_map/pallas_call | solution.py:606
  19.8 0.7 %shard_map.87 = (f32[32,128]{1,0:T(8,128)}, f32[4,32,128]{2,1,0:T(8,128)}) custom-call(f32[32,128]{1,0:T(8,128)S(1)} %get-tuple-element.4.dens_ref, f32[4,32,128]{2,1,0:T(8,128)S(1)} %get-tuple-element.5.rest_ref), custom_call_target="tpu_custom_call" | custom-call | tf_op jit(solution)/shard_map/pallas_call | solution.py:655

commit v5 on v4

--- a/solution.py
+++ b/solution.py
@@ -455,6 +455,7 @@
         return summed
 
     lane = iota((slab_x, slab_y), 1)
+    line_id = iota((slab_x, slab_y), 0)
 
     def edges_of(origin):
         x, y = origin
@@ -471,7 +472,7 @@
             src_ref=out_ref.at[phase, side],
             dst_ref=in_ref.at[phase, side],
             send_sem=load_sem.at[at],
-            recv_sem=halo_recv.at[at],
+            recv_sem=halo_recv.at[0],
             device_id=target,
             device_id_type=MESH,
         )
@@ -548,29 +549,47 @@
     lax.fori_loop(0, 2 * groups, step, 0)
     mine = deposit_of(1)
     far_copy(far_out, far_in, 1).wait_recv()
-    for phase in range(2):
-        for out_ref, in_ref, side, base, target, sends, takes in edges_of(origins[1]):
-
-            @pl.when(takes)
-            def _():
-                edge(phase, out_ref, in_ref, side, base, target).wait_recv()
-
-    rows_in = [row_in[0, side] + row_in[1, side] for side in range(2)]
+    nothing = jnp.zeros((1, slab_y), F32)
+
+    def out_of(c):
+        return rest_out.at[c - 1] if c else dens_out
+
+    for c in range(5):
+        here = mine[c] + far_in[c]
+        beside = jnp.concatenate([nothing, here[: slab_x - 1]], axis=0)
+        beside += jnp.concatenate([here[1:], nothing], axis=0)
+        beside += jnp.where(lane == 0, 0.0, pltpu.roll(here, 1, 1))
+        beside += jnp.where(lane == slab_y - 1, 0.0, pltpu.roll(here, slab_y - 1, 1))
+        out_of(c)[...] = field[c] + (0.4 * here + 0.15 * beside)
+
+    takers = sum(jnp.where(takes, 1, 0) for *_, takes in edges_of(origins[1]))
+    for count in range(1, 5):
+
+        @pl.when(takers == count)
+        def _():
+            strips = got.at[0, pl.ds(0, 2 * count * ROWS)]
+            pltpu.make_async_remote_copy(
+                src_ref=strips,
+                dst_ref=strips,
+                send_sem=send_sem.at[0],
+                recv_sem=halo_recv.at[0],
+                device_id=mirror,
+                device_id_type=MESH,
+            ).wait_recv()
+
+    rows_in = [0.15 * (row_in[0, side] + row_in[1, side]) for side in range(2)]
     cols_in = [
-        jnp.transpose(col_in[0, side] + col_in[1, side])[:slab_x] for side in range(2)
+        jnp.transpose(0.15 * (col_in[0, side] + col_in[1, side]))[:slab_x]
+        for side in range(2)
     ]
     for c in range(5):
-        here = mine[c] + far_in[c]
-        above = jnp.concatenate([rows_in[1][c : c + 1], here[: slab_x - 1]], axis=0)
-        below = jnp.concatenate([here[1:], rows_in[0][c : c + 1]], axis=0)
         beside = [jnp.broadcast_to(x[:, c : c + 1], (slab_x, slab_y)) for x in cols_in]
-        left = jnp.where(lane == 0, beside[1], pltpu.roll(here, 1, 1))
-        right = jnp.where(lane == slab_y - 1, beside[0], pltpu.roll(here, slab_y - 1, 1))
-        smooth = 0.4 * here + 0.15 * (below + above + right + left)
-        if c:
-            rest_out[c - 1] = field[c] + smooth
-        else:
-            dens_out[...] = field[0] + smooth
+        sides = jnp.where(
+            lane == 0, beside[1], jnp.where(lane == slab_y - 1, beside[0], 0.0)
+        )
+        sides += jnp.where(line_id == 0, rows_in[1][c : c + 1], 0.0)
+        sides += jnp.where(line_id == slab_x - 1, rows_in[0][c : c + 1], 0.0)
+        out_of(c)[...] += sides
 
     for phase in range(2):
         blocks = packed.at[phase, pl.ds(0, team - 1)]
@@ -640,7 +659,7 @@
             pltpu.SemaphoreType.DMA((2, team // ROWS)),
             pltpu.SemaphoreType.DMA((2,)),
             pltpu.SemaphoreType.DMA((2,)),
-            pltpu.SemaphoreType.DMA((8,)),
+            pltpu.SemaphoreType.DMA((1,)),
         ],
         compiler_params=pltpu.CompilerParams(collective_id=0, has_side_effects=True),
     )(

time: 20.7 us -> 20.6 us (level)
  no operation moved by 1% of the time
where the time goes in v5:
time: 20.6 us; the launch traced here: 20.4 us
  Pallas kernels  19.7 us (96%)
  between operations  0.64 us (3%)
    pallas_call x1, Pallas kernels, per_device(): pl.pallas_call(functools.partial(fused_kernel, width_x, width_y, capacity...  19.1 us
    pallas_call x1, Pallas kernels, per_device(): pl.pallas_call(store_kernel, out_shape=(jax.ShapeDtypeStruct(dens.shape,...  0.65 us

profile of v5, /device:TPU:0, one launch (start us, length us, event | category | flops | bytes accessed | tf_op | source)
XLA Modules:
  0.0 20.4 jit_solution(6609522721393301174)
XLA Ops:
  0.6 19.1 %shard_map.86 = (f32[32,128]{1,0:T(8,128)S(1)}, f32[4,32,128]{2,1,0:T(8,128)S(1)}) custom-call(f32[16,4096]{1,0:T(8,128)} %props_hbm.1, s32[1,4096]{1,0:T(1,128)} %bitcast.3, s32[1,4096]{1,0:T(1,128)} %bitcast.4, s32[1,4096]{1,0:T(1,128)} %bitcast.5, f32[8,16]{1,0:T(8,128)} %table_hbm.1, f32[32,128]{1,0:T(8,128)} %dens_hbm.1, f32[4,32,128]{2,1,0:T(8,128)} %rest_hbm.1), custom_call_target="tpu_custom_call" | custom-call | tf_op jit(solution)/shard_map/pallas_call | solution.py:625
  19.7 0.7 %shard_map.87 = (f32[32,128]{1,0:T(8,128)}, f32[4,32,128]{2,1,0:T(8,128)}) custom-call(f32[32,128]{1,0:T(8,128)S(1)} %get-tuple-element.4.dens_ref, f32[4,32,128]{2,1,0:T(8,128)S(1)} %get-tuple-element.5.rest_ref), custom_call_target="tpu_custom_call" | custom-call | tf_op jit(solution)/shard_map/pallas_call | solution.py:674

commit v6 on v5

--- a/solution.py
+++ b/solution.py
@@ -536,13 +536,13 @@
                 far_out[c] = deposit[c]
             send_edges(0, deposit)
 
+        @pl.when(t == far_stop + hold)
+        def _():
+            far_copy(far_out, far_in, 1).start()
+
         @pl.when(t == own_stop)
         def _():
             send_edges(1, deposit_of(1))
-
-        @pl.when(t == far_stop + hold)
-        def _():
-            far_copy(far_out, far_in, 1).start()
 
         return unused
 

time: 20.6 us -> 20.6 us (level)
  no operation moved by 1% of the time
where the time goes in v6:
time: 20.6 us; the launch traced here: 20.4 us
  Pallas kernels  19.7 us (96%)
  between operations  0.64 us (3%)
    pallas_call x1, Pallas kernels, per_device(): pl.pallas_call(functools.partial(fused_kernel, width_x, width_y, capacity...  19.1 us
    pallas_call x1, Pallas kernels, per_device(): pl.pallas_call(store_kernel, out_shape=(jax.ShapeDtypeStruct(dens.shape,...  0.65 us

profile of v6, /device:TPU:0, one launch (start us, length us, event | category | flops | bytes accessed | tf_op | source)
XLA Modules:
  0.0 20.4 jit_solution(5276393250179476115)
XLA Ops:
  0.6 19.1 %shard_map.86 = (f32[32,128]{1,0:T(8,128)S(1)}, f32[4,32,128]{2,1,0:T(8,128)S(1)}) custom-call(f32[16,4096]{1,0:T(8,128)} %props_hbm.1, s32[1,4096]{1,0:T(1,128)} %bitcast.3, s32[1,4096]{1,0:T(1,128)} %bitcast.4, s32[1,4096]{1,0:T(1,128)} %bitcast.5, f32[8,16]{1,0:T(8,128)} %table_hbm.1, f32[32,128]{1,0:T(8,128)} %dens_hbm.1, f32[4,32,128]{2,1,0:T(8,128)} %rest_hbm.1), custom_call_target="tpu_custom_call" | custom-call | tf_op jit(solution)/shard_map/pallas_call | solution.py:625
  19.7 0.7 %shard_map.87 = (f32[32,128]{1,0:T(8,128)}, f32[4,32,128]{2,1,0:T(8,128)}) custom-call(f32[32,128]{1,0:T(8,128)S(1)} %get-tuple-element.4.dens_ref, f32[4,32,128]{2,1,0:T(8,128)S(1)} %get-tuple-element.5.rest_ref), custom_call_target="tpu_custom_call" | custom-call | tf_op jit(solution)/shard_map/pallas_call | solution.py:674
